TPU v7x, 32 devices: a whole 2x2x4 slice. The times are simulated.
32 devices in a mesh: rows: 32 (over z, y, x, core).
Axes of the slice: x: 2, y: 2, z: 4, core: 2. Of those that a mesh axis runs over, the one named last changes fastest.
Arguments:
- tile_values: float32 [3584, 128, 128], P('rows'), as said below
- tile_row: int32 [3584], P('rows'), may hold values from 0 to 15, as said below
- tile_slot: int32 [3584], P('rows'), may hold values from 0 to 47, as said below
- tile_count: int32 [32], P('rows'), may hold values from 48 to 112, as said below
- requests: int32 [32, 32, 1], P('rows'), may hold values from 0 to 15
- right_side: float32 [512, 4, 128], P('rows')
Outputs:
- solution: float32 [512, 4, 128], P('rows')
- hessenberg: float32 [4, 4, 3], replicated
Inputs may be any that keep to these rules, and one draw needn't show every extreme that they name: `tile_row`: tile t < 16 of every device lies in block row t; it is the diagonal tile of that row. `tile_slot`: slot s < 16 is the device's own block s; slot 16 + o + q is the q-th block requested from device o; tile t < 48 of every device uses slot t. `tile_count`: some device uses all 112 slots. requests[d, o, q] is a block index among device o's 16 block rows. `tile_values`: tile t < 16 of every device holds the diagonal block of its row.
All inputs are finite; a program needn't handle non-finite values.
Results may differ from a plain program's by a relative error of at most 0.0003.
Values sent between devices are 32-bit elements; how exact they have to be, the bound alone decides.
A program may use at most 64 MiB of HBM per device.

v0:
```python
import functools

import jax
import jax.numpy as jnp
from jax import lax
from jax.experimental import pallas as pl
from jax.experimental.pallas import tpu as pltpu
from jax.sharding import PartitionSpec as P

ITERS = 3
MESH = pl.DeviceIdType.MESH
epsilon = 1e-06
f32 = jnp.float32
bf16 = jnp.bfloat16


def split(x):
    high = x.astype(bf16).astype(f32)
    return high, x - high


def dot(a, b):
    return lax.dot_general(a, b, (((1,), (0,)), ((), ())), preferred_element_type=f32)


def twice(x):
    return jnp.concatenate([x, x], axis=0)


def kernel(
    n,
    chunk,
    unroll,
    tile_hbm,
    row_ref,
    count_ref,
    slot_ref,
    request_ref,
    right_ref,
    out_ref,
    hess_ref,
    tiles,
    parts,
    selector,
    spread,
    asked,
    outgoing,
    incoming,
    own,
    slots,
    table,
    products,
    tile_sem,
    ask_send,
    ask_recv,
    send_sem,
    recv_sem,
):
    me = lax.axis_index("rows")
    total, size, _ = tiles.shape
    blocks, systems, _ = right_ref.shape
    rows = 2 * systems
    chunks = total // chunk
    batch = max(b for b in range(1, 57) if total % b == 0)

    def tile_copy(index):
        where = pl.ds(index * chunk, chunk)
        return pltpu.make_async_copy(tile_hbm.at[where], tiles.at[where], tile_sem.at[index])

    for index in range(chunks):
        tile_copy(index).start()

    def peer_of(step):
        return lax.rem(me + step, n)

    def each_peer(body):
        def run(step, carry):
            body(step, peer_of(step))
            return carry

        lax.fori_loop(1, n, run, 0, unroll=min(unroll, n - 1))

    barrier = pltpu.get_barrier_semaphore()
    each_peer(
        lambda step, peer: pl.semaphore_signal(
            barrier, inc=1, device_id=(peer,), device_id_type=MESH
        )
    )

    lane = lax.broadcasted_iota(jnp.int32, (1, total), 1)
    live_row = jnp.where(lane < count_ref[...], row_ref[...], blocks)
    wide = total * rows
    from_tile = lax.broadcasted_iota(jnp.int32, (total, wide), 0)
    to_column = lax.broadcasted_iota(jnp.int32, (total, wide), 1)
    expand = jnp.where(to_column // rows == from_tile, 1.0, 0.0).astype(bf16)
    row_of = dot(jnp.broadcast_to(live_row.astype(f32), (8, total)).astype(bf16), expand)[0:1]
    for block in range(blocks):
        k_row = lax.broadcasted_iota(jnp.int32, (rows, wide), 0)
        q_col = lax.broadcasted_iota(jnp.int32, (rows, wide), 1)
        fits = (k_row % systems == q_col % systems) & (
            jnp.broadcast_to(row_of, (rows, wide)) == float(block)
        )
        spread[pl.ds(block * rows, rows), :] = jnp.where(fits, 1.0, 0.0)
    selector[...] = spread[...].astype(bf16)

    for block in range(blocks):
        own[0, block] = twice(right_ref[block])

    pl.semaphore_wait(barrier, n - 1)

    def ask_copy(step, peer):
        return pltpu.make_async_remote_copy(
            src_ref=request_ref,
            dst_ref=asked.at[me],
            send_sem=ask_send.at[step],
            recv_sem=ask_recv.at[me],
            device_id=(peer,),
            device_id_type=MESH,
        )

    def ask_arrival(peer):
        return pltpu.make_async_remote_copy(
            src_ref=request_ref,
            dst_ref=asked.at[peer],
            send_sem=ask_send.at[0],
            recv_sem=ask_recv.at[peer],
            device_id=(peer,),
            device_id_type=MESH,
        )

    each_peer(lambda step, peer: ask_copy(step, peer).start())

    def split_chunk(index, carry):
        tile_copy(index).wait()

        def split_tile(offset, carry):
            tile = index * chunk + offset
            high, low = split(tiles[tile].T)
            parts[tile, 0:size, :] = high.astype(bf16)
            parts[tile, size : 2 * size, :] = low.astype(bf16)
            return carry

        return lax.fori_loop(0, chunk, split_tile, carry, unroll=4)

    lax.fori_loop(0, chunks, split_chunk, 0)

    each_peer(lambda step, peer: ask_arrival(peer).wait_recv())
    each_peer(lambda step, peer: ask_copy(step, peer).wait_send())

    sub = lax.broadcasted_iota(jnp.int32, (rows, size), 0)
    lanes = lax.broadcasted_iota(jnp.int32, (rows, size), 1)
    system_of = sub % systems

    def message(parity, step, peer):
        return pltpu.make_async_remote_copy(
            src_ref=outgoing.at[parity, peer, pl.ds(0, systems + 1)],
            dst_ref=incoming.at[parity, me, pl.ds(0, systems + 1)],
            send_sem=send_sem.at[parity, peer],
            recv_sem=recv_sem.at[parity, me],
            device_id=(peer,),
            device_id_type=MESH,
        )

    def arrival(parity, peer):
        return pltpu.make_async_remote_copy(
            src_ref=outgoing.at[parity, peer, pl.ds(0, systems + 1)],
            dst_ref=incoming.at[parity, peer, pl.ds(0, systems + 1)],
            send_sem=send_sem.at[parity, peer],
            recv_sem=recv_sem.at[parity, peer],
            device_id=(peer,),
            device_id_type=MESH,
        )

    def exchange(parity, vector, sums):
        packed = jnp.zeros((rows, size), f32)
        for position, entry in enumerate(sums):
            packed = packed + jnp.where(lanes == rows * position + sub, entry, 0.0)
        packed = jnp.sum(packed[0:systems], axis=0, keepdims=True)
        incoming[parity, me, pl.ds(systems, 1), :] = packed

        def send(step, peer):
            outgoing[parity, peer, pl.ds(0, systems), :] = own[vector, asked[peer, 0, me]][0:systems]
            outgoing[parity, peer, pl.ds(systems, 1), :] = packed
            message(parity, step, peer).start()

        each_peer(send)

    def arrive(parity, count):
        each_peer(lambda step, peer: arrival(parity, peer).wait_recv())
        each_peer(lambda step, peer: message(parity, step, peer).wait_send())
        whole = jnp.sum(incoming[parity, :, systems, :], axis=0, keepdims=True)
        whole = jnp.broadcast_to(whole, (rows, size))
        return [
            jnp.broadcast_to(
                jnp.sum(
                    jnp.where(lanes == rows * position + system_of, whole, 0.0),
                    axis=1,
                    keepdims=True,
                ),
                (rows, size),
            )
            for position in range(count)
        ]

    def local_sum(x, y):
        return jnp.sum(jnp.sum(x * y, axis=0), axis=1, keepdims=True)

    def multiply():
        def step(group, carry):
            for offset in range(batch):
                tile = group * batch + offset
                x = table[slot_ref[tile]].astype(bf16)
                y = dot(jnp.concatenate([x, x], axis=1), parts[tile])
                products[pl.ds(pl.multiple_of(tile * rows, rows), rows), :] = y
            return carry

        lax.fori_loop(0, total // batch, step, 0)
        high, low = split(products[...])
        result = dot(selector[...], high.astype(bf16)) + dot(selector[...], low.astype(bf16))
        return result.reshape(blocks, rows, size)

    def fill(index, scale, coefficients, parity):
        def place(slot, raw):
            for earlier, value in enumerate(coefficients):
                raw = raw - value * slots[earlier, slot]
            raw = raw * scale
            slots[index, slot] = raw
            high, low = split(raw)
            table[slot] = jnp.where(sub < systems, high, low)

        for block in range(blocks):
            place(block, own[index, block])

        def run(peer, carry):
            place(blocks + peer, twice(incoming[parity, peer, pl.ds(0, systems), :]))
            return carry

        lax.fori_loop(0, n, run, 0, unroll=min(8, n))

    def keep_own(parity, vector):
        incoming[parity, me, pl.ds(0, systems), :] = own[vector, request_ref[0, me]][0:systems]

    zero = jnp.zeros((rows, size), f32)
    right = own[0]
    exchange(0, 0, [local_sum(right, right)])
    keep_own(0, 0)
    (square,) = arrive(0, 1)
    beta = jnp.sqrt(square + epsilon)
    scale = 1.0 / beta
    gram = {(0, 0): square * scale * scale}
    coefficients = []
    triangle = []
    raw_columns = []
    rotations = []
    target = [beta]
    parity = 0
    for column in range(ITERS):
        fill(column, scale, coefficients, parity)
        candidate = multiply()
        parity = (column + 1) % 2
        sums = [local_sum(candidate, slots[i, 0:blocks]) for i in range(column + 1)]
        sums.append(local_sum(candidate, candidate))
        if column + 1 < ITERS:
            own[column + 1] = candidate
            exchange(parity, column + 1, sums)
            keep_own(parity, column + 1)
        else:
            own[ITERS] = candidate
            exchange(parity, column + 1, sums)
        if column >= 1:
            rotate(raw_columns[column - 1], rotations, triangle, target)
        summed = arrive(parity, column + 2)

        def inner(i, j):
            return gram[(min(i, j), max(i, j))]

        coefficients = []
        for i in range(column + 1):
            value = summed[i]
            for earlier in range(i):
                value = value - coefficients[earlier] * inner(earlier, i)
            coefficients.append(value)
        residual = summed[column + 1]
        for i in range(column + 1):
            residual = residual - 2.0 * coefficients[i] * summed[i]
        for i in range(column + 1):
            for j in range(column + 1):
                residual = residual + coefficients[i] * coefficients[j] * inner(i, j)
        residual = jnp.maximum(residual, 0.0)
        length = jnp.sqrt(residual + epsilon)
        scale = 1.0 / length
        if column + 1 < ITERS:
            for i in range(column + 1):
                value = summed[i]
                for earlier in range(column + 1):
                    value = value - coefficients[earlier] * inner(earlier, i)
                gram[(i, column + 1)] = value * scale
            gram[(column + 1, column + 1)] = residual * scale * scale
        raw_columns.append(coefficients + [length])
    rotate(raw_columns[ITERS - 1], rotations, triangle, target)
    weights = [None] * ITERS
    for column in reversed(range(ITERS)):
        value = target[column]
        for later in range(column + 1, ITERS):
            value = value - triangle[later][column] * weights[later]
        weights[column] = value / triangle[column][column]
    solved = weights[0] * slots[0, 0:blocks]
    for i in range(1, ITERS):
        solved = solved + weights[i] * slots[i, 0:blocks]
    for block in range(blocks):
        out_ref[block] = solved[block, 0:systems]
    for column in range(ITERS):
        picture = zero
        for i in range(column + 2):
            picture = jnp.where(lanes == i, raw_columns[column][i], picture)
        hess_ref[column] = picture[0:systems, 0 : ITERS + 1]


def rotate(column, rotations, triangle, target):
    column = list(column)
    for i, (cosine, sine) in enumerate(rotations):
        first, second = column[i], column[i + 1]
        column[i] = cosine * first + sine * second
        column[i + 1] = cosine * second - sine * first
    last = len(column) - 2
    first, second = column[last], column[last + 1]
    radius = jnp.sqrt(first * first + second * second)
    cosine, sine = first / radius, second / radius
    rotations.append((cosine, sine))
    column[last] = radius
    triangle.append(column[: last + 1])
    leading = target[last]
    target[last] = cosine * leading
    target.append(-sine * leading)


def hand_on(solved_ref, picture_ref, out_ref, hess_ref):
    out_ref[...] = solved_ref[...]
    hess_ref[...] = picture_ref[...]


def on_device(tile_values, tile_row, tile_slot, tile_count, requests, right_side):
    n = lax.axis_size("rows")
    total, size, _ = tile_values.shape
    blocks, systems, _ = right_side.shape
    rows = 2 * systems
    chunk = 16 if total % 16 == 0 else 1
    smem = pl.BlockSpec(memory_space=pltpu.SMEM)
    vmem = pl.BlockSpec(memory_space=pltpu.VMEM)
    dma = pltpu.SemaphoreType.DMA
    solved, picture = pl.pallas_call(
        functools.partial(kernel, n, chunk, 8),
        out_shape=(
            jax.ShapeDtypeStruct((blocks, systems, size), f32),
            jax.ShapeDtypeStruct((ITERS, systems, ITERS + 1), f32),
        ),
        in_specs=[pl.BlockSpec(memory_space=pl.ANY), vmem, vmem, smem, smem, vmem],
        out_specs=(vmem, vmem),
        scratch_shapes=[
            pltpu.VMEM((total, size, size), f32),
            pltpu.VMEM((total, 2 * size, size), bf16),
            pltpu.VMEM((blocks * rows, total * rows), bf16),
            pltpu.VMEM((blocks * rows, total * rows), f32),
            pltpu.SMEM((n, 1, n), jnp.int32),
            pltpu.VMEM((2, n, 8, size), f32),
            pltpu.VMEM((2, n, 8, size), f32),
            pltpu.VMEM((ITERS + 1, blocks, rows, size), f32),
            pltpu.VMEM((ITERS, blocks + n, rows, size), f32),
            pltpu.VMEM((blocks + n, rows, size), f32),
            pltpu.VMEM((total * rows, size), f32),
            dma((total // chunk,)),
            dma((n,)),
            dma((n,)),
            dma((2, n)),
            dma((2, n)),
        ],
        compiler_params=pltpu.CompilerParams(
            collective_id=0, has_side_effects=True, vmem_limit_bytes=60 * 1024 * 1024
        ),
        name="cycle",
    )(
        tile_values,
        tile_row.reshape(1, total),
        tile_count.reshape(1, 1),
        tile_slot,
        requests.reshape(1, n),
        right_side,
    )
    solved, picture = pl.pallas_call(
        hand_on,
        out_shape=(
            jax.ShapeDtypeStruct(solved.shape, f32),
            jax.ShapeDtypeStruct(picture.shape, f32),
        ),
        in_specs=[vmem, vmem],
        out_specs=(vmem, vmem),
        name="hand_on",
    )(solved, picture)
    return solved, jnp.transpose(picture, (1, 2, 0))


def solution(mesh):
    return jax.shard_map(
        on_device,
        mesh=mesh,
        in_specs=(
            P("rows", None, None),
            P("rows"),
            P("rows"),
            P("rows"),
            P("rows", None, None),
            P("rows", None, None),
        ),
        out_specs=(P("rows", None, None), P()),
        check_vma=False,
    )
```

profile of v0, /device:TPU:0, one launch (start us, length us, event | category | flops | bytes accessed | tf_op | source)
XLA Modules:
  0.0 43.2 jit_solution(12440944111916769189)
XLA Ops:
  1.3 40.5 %cycle.1 = (f32[16,4,128]{2,1,0:T(4,128)}, f32[3,4,4]{2,1,0:T(4,128)}) custom-call(f32[112,128,128]{2,1,0:T(8,128)} %tile_hbm.1, s32[1,112]{1,0:T(1,128)} %bitcast.5, s32[1,1]{1,0:T(1,128)} %bitcast.4.count_ref, s32[112]{0:T(128)} %slot_ref.1, s32[1,32]{1,0:T(1,128)} %bitcast.6, f32[16,4,128]{2,1,0:T(4,128)} %right_ref.1), custom_call_target="tpu_custom_call" | custom-call | tf_op jit(solution)/shard_map/cycle/pallas_call | solution.py:351
  41.8 1.4 %hand_on.1 = (f32[16,4,128]{2,1,0:T(4,128)}, f32[3,4,4]{2,1,0:T(4,128)}) custom-call(f32[16,4,128]{2,1,0:T(4,128)} %get-tuple-element.6.solved_ref, f32[3,4,4]{2,1,0:T(4,128)} %get-tuple-element.7.picture_ref), custom_call_target="tpu_custom_call" | custom-call | tf_op jit(solution)/shard_map/hand_on/pallas_call | solution.py:389
where the time goes:
time: 43.4 us; the launch traced here: 43.2 us
  Pallas kernels  41.9 us (97%)
  between operations  1.28 us (3%)
    pallas_call x1, Pallas kernels, on_device(): pl.pallas_call(functools.partial(kernel, n, chunk, 8), out_shape=(jax.Sha...  40.5 us
    pallas_call x1, Pallas kernels, on_device(): pl.pallas_call(hand_on, out_shape=(jax.ShapeDtypeStruct(solved.shape, f32...  1.38 us

commit v1 on v0

v1 whole, which is shorter than its diff:
```python
import functools

import jax
import jax.numpy as jnp
from jax import lax
from jax.experimental import pallas as pl
from jax.experimental.pallas import tpu as pltpu
from jax.sharding import PartitionSpec as P

ITERS = 3
MESH = pl.DeviceIdType.MESH
epsilon = 1e-06
f32 = jnp.float32
bf16 = jnp.bfloat16


def split(x):
    high = x.astype(bf16).astype(f32)
    return high, x - high


def dot(a, b):
    return lax.dot_general(a, b, (((1,), (0,)), ((), ())), preferred_element_type=f32)


def twice(x):
    return jnp.concatenate([x, x], axis=0)


def flip(value, mask, bits):
    result = 0
    for bit in range(bits):
        a = lax.rem(value // 2**bit, 2)
        b = mask // 2**bit % 2 if isinstance(mask, int) else lax.rem(mask // 2**bit, 2)
        result = result + (a + b - 2 * a * b) * 2**bit
    return result


def kernel(
    n,
    low,
    chunk,
    early,
    tile_hbm,
    row_hbm,
    count_hbm,
    slot_hbm,
    request_hbm,
    right_hbm,
    out_ref,
    hess_ref,
    tiles,
    parts,
    selector,
    row_ref,
    count_ref,
    slot_ref,
    request_ref,
    asked,
    outgoing,
    incoming,
    sums_out,
    sums_in,
    own,
    basis,
    table,
    highs,
    lows,
    tile_sem,
    load_sem,
    ask_send,
    ask_recv,
    send_sem,
    recv_sem,
    sums_send,
    sums_recv,
):
    me = lax.axis_index("rows")
    total, size, _ = tiles.shape
    _, height, _ = own.shape
    systems = outgoing.shape[2]
    blocks = height // systems
    rows = 2 * systems
    statics = blocks + n
    chunks = total // chunk
    far = n // low
    far_bits, low_bits = far.bit_length() - 1, low.bit_length() - 1
    group_of_me, place = me // low, lax.rem(me, low)
    beside = [flip(place, step, low_bits) for step in range(low)]

    def across(step):
        if far == 2**far_bits:
            return flip(group_of_me, step, far_bits) * low
        return lax.rem(group_of_me + step, far) * low

    home = group_of_me * low

    def far_first(body):
        def run(index, carry):
            group = across(far - 1 - index)
            for step in reversed(range(low)):
                body(group + beside[step])
            return carry

        lax.fori_loop(0, far - 1, run, 0, unroll=min(3, far - 1))
        for step in reversed(range(1, low)):
            body(home + beside[step])

    def remote(source, target, send, recv, peer):
        return pltpu.make_async_remote_copy(
            src_ref=source,
            dst_ref=target,
            send_sem=send,
            recv_sem=recv,
            device_id=(peer,),
            device_id_type=MESH,
        )

    barrier = pltpu.get_barrier_semaphore()
    far_first(
        lambda peer: pl.semaphore_signal(barrier, inc=1, device_id=(peer,), device_id_type=MESH)
    )

    def tile_copy(index):
        where = pl.ds(index * chunk, chunk)
        return pltpu.make_async_copy(tile_hbm.at[where], tiles.at[where], tile_sem.at[index])

    loads = [
        pltpu.make_async_copy(source, target, load_sem.at[index])
        for index, (source, target) in enumerate(
            [
                (request_hbm, request_ref),
                (row_hbm, row_ref),
                (count_hbm, count_ref),
                (slot_hbm, slot_ref),
                (right_hbm, own.at[0]),
            ]
        )
    ]
    for load in loads:
        load.start()
    for index in range(chunks):
        tile_copy(index).start()

    def split_chunk(index, carry):
        tile_copy(index).wait()

        def split_tile(offset, carry):
            tile = index * chunk + offset
            high, low_part = split(tiles[tile].T)
            parts[tile, 0:size, :] = high.astype(bf16)
            parts[tile, size : 2 * size, :] = low_part.astype(bf16)
            return carry

        return lax.fori_loop(0, chunk, split_tile, carry, unroll=4)

    lax.fori_loop(0, early, split_chunk, 0)
    pl.semaphore_wait(barrier, n - 1)
    for load in loads:
        load.wait()
    far_first(
        lambda peer: remote(request_ref, asked.at[me], ask_send, ask_recv, peer).start()
    )
    lax.fori_loop(early, chunks, split_chunk, 0)

    lane = lax.broadcasted_iota(jnp.int32, (1, total), 1)
    live_row = jnp.where(lane < count_ref[0], row_ref[...], blocks)
    wide = total * rows
    from_tile = lax.broadcasted_iota(jnp.int32, (total, wide), 0)
    to_column = lax.broadcasted_iota(jnp.int32, (total, wide), 1)
    expand = jnp.where(to_column // rows == from_tile, 1.0, 0.0).astype(bf16)
    row_of = dot(jnp.broadcast_to(live_row.astype(f32), (8, total)).astype(bf16), expand)[0:1]
    for pair in range(blocks // 2):
        k_row = lax.broadcasted_iota(jnp.int32, (rows, wide), 0)
        q_col = lax.broadcasted_iota(jnp.int32, (rows, wide), 1)
        block = (2 * pair + k_row // systems).astype(f32)
        fits = (k_row % systems == q_col % systems) & (
            jnp.broadcast_to(row_of, (rows, wide)) == block
        )
        selector[pl.ds(pair * rows, rows), :] = jnp.where(fits, 1.0, 0.0)

    sub = lax.broadcasted_iota(jnp.int32, (rows, size), 0)
    lanes = lax.broadcasted_iota(jnp.int32, (rows, size), 1)
    system_of = sub % systems

    def send_blocks(column):
        def send(peer):
            start = asked[peer, 0, me] * systems
            outgoing[column, peer] = own[column, pl.ds(start, systems), :]
            remote(
                outgoing.at[column, peer],
                incoming.at[column, me],
                send_sem.at[column],
                recv_sem.at[column, me],
                peer,
            ).start()

        far_first(send)

    def fold(x, y):
        product = (x * y).reshape(height // rows, rows, size)
        return jnp.sum(jnp.sum(product, axis=0), axis=1, keepdims=True)

    def send_sums(turn, sums):
        packed = jnp.zeros((rows, size), f32)
        for position, entry in enumerate(sums):
            packed = packed + jnp.where(lanes == rows * position + sub, entry, 0.0)
        packed = jnp.sum(packed, axis=0, keepdims=True)
        sums_out[turn] = packed
        sums_in[turn, me] = packed
        far_first(
            lambda peer: remote(
                sums_out.at[turn],
                sums_in.at[turn, me],
                sums_send.at[turn],
                sums_recv.at[turn],
                peer,
            ).start()
        )

    def all_sums(turn):
        others = pl.ds(0, n - 1)
        return remote(
            sums_in.at[turn, others],
            sums_in.at[turn, others],
            sums_send.at[turn],
            sums_recv.at[turn],
            home + beside[1],
        )

    def arrive_sums(turn, count):
        all_sums(turn).wait_recv()
        whole = jnp.sum(sums_in[turn], axis=0)
        whole = jnp.broadcast_to(whole, (rows, size))
        return [
            jnp.broadcast_to(
                jnp.sum(
                    jnp.where(
                        (lanes // rows == position) & (lanes % systems == system_of), whole, 0.0
                    ),
                    axis=1,
                    keepdims=True,
                ),
                (rows, size),
            )
            for position in range(count)
        ]

    def fill(slot, raw):
        high, rest = split(twice(raw))
        table[slot] = jnp.where(sub < systems, high, rest)

    def multiply(first, count):
        for pair in range(count // 2):
            both = []
            for side in range(2):
                tile, slot = first(2 * pair + side)
                x = table[slot].astype(bf16)
                both.append(dot(jnp.concatenate([x, x], axis=1), parts[tile]))
            y = jnp.concatenate(both, axis=0)
            high, rest = split(y)
            tile, _ = first(2 * pair)
            where = pl.ds(pl.multiple_of(tile * rows, 2 * rows), 2 * rows)
            highs[where, :] = high.astype(bf16)
            lows[where, :] = rest.astype(bf16)

    def near_tiles(column):
        for block in range(blocks):
            fill(block, own[column, pl.ds(block * systems, systems), :])
        multiply(lambda index: (index, index), blocks)

    def group_tiles(column, step):
        group = across(step)
        for index in range(low):
            fill(blocks + group + index, incoming[column, group + index])
        multiply(lambda index: (blocks + group + index, blocks + group + index), low)

    def arrive(column, step, skip):
        group = across(step)
        for index in range(skip, low):
            peer = group + beside[index]
            remote(
                outgoing.at[column, peer],
                incoming.at[column, peer],
                send_sem.at[column],
                recv_sem.at[column, peer],
                peer,
            ).wait_recv()

    def static_tiles(column):
        near_tiles(column)
        incoming[column, me] = own[column, pl.ds(request_ref[0, me] * systems, systems), :]
        arrive(column, 0, 1)
        group_tiles(column, 0)

        def run(step, carry):
            arrive(column, step, 0)
            group_tiles(column, step)
            return carry

        lax.fori_loop(1, far, run, 0, unroll=min(3, far - 1))

    def select():
        pick = selector[...].astype(bf16)
        return dot(pick, highs[...]) + dot(pick, lows[...])

    def spread(value):
        return jnp.tile(value, (height // rows, 1))

    zero = jnp.zeros((rows, size), f32)
    remote(asked.at[pl.ds(0, n - 1)], asked.at[pl.ds(0, n - 1)], ask_send, ask_recv, home).wait_recv()
    send_blocks(0)
    send_sums(0, [fold(own[0], own[0])])

    gram = {}
    triangle = []
    raw_columns = []
    rotations = []
    target = []
    coefficients = []
    extras = total - statics
    half = extras // 4 * 2

    def inner(i, j):
        return gram[(min(i, j), max(i, j))]

    def orthogonalize(column, summed):
        if column == 0:
            beta = jnp.sqrt(summed[0] + epsilon)
            scale = 1.0 / beta
            gram[(0, 0)] = summed[0] * scale * scale
            target.append(beta)
            return [], scale
        count = column
        values = []
        for i in range(count):
            value = summed[i]
            for earlier in range(i):
                value = value - values[earlier] * inner(earlier, i)
            values.append(value)
        residual = summed[count]
        for i in range(count):
            residual = residual - 2.0 * values[i] * summed[i]
        for i in range(count):
            for j in range(count):
                residual = residual + values[i] * values[j] * inner(i, j)
        residual = jnp.maximum(residual, 0.0)
        length = jnp.sqrt(residual + epsilon)
        scale = 1.0 / length
        if column < ITERS:
            for i in range(count):
                value = summed[i]
                for earlier in range(count):
                    value = value - values[earlier] * inner(earlier, i)
                gram[(i, count)] = value * scale
            gram[(count, count)] = residual * scale * scale
        raw_columns.append(values + [length])
        return values, scale

    for column in range(ITERS):
        static_tiles(column)
        multiply(lambda index: (statics + index, slot_ref[statics + index]), half)
        summed = arrive_sums(column, column + 1)
        values, scale = orthogonalize(column, summed)
        vector = own[column]
        for i, value in enumerate(values):
            vector = vector - spread(value) * basis[i]
        vector = vector * spread(scale)
        basis[column] = vector
        multiply(
            lambda index: (statics + half + index, slot_ref[statics + half + index]),
            extras - half,
        )
        candidate = select()
        for i, value in enumerate(values):
            candidate = candidate - spread(value) * own[i + 1]
        candidate = candidate * spread(scale)
        own[column + 1] = candidate
        if column + 1 < ITERS:
            send_blocks(column + 1)
        sums = [fold(candidate, basis[i]) for i in range(column + 1)]
        sums.append(fold(candidate, candidate))
        send_sums(column + 1, sums)
        if column >= 1:
            rotate(raw_columns[column - 1], rotations, triangle, target)

    summed = arrive_sums(ITERS, ITERS + 1)
    orthogonalize(ITERS, summed)
    rotate(raw_columns[ITERS - 1], rotations, triangle, target)
    weights = [None] * ITERS
    for column in reversed(range(ITERS)):
        value = target[column]
        for later in range(column + 1, ITERS):
            value = value - triangle[later][column] * weights[later]
        weights[column] = value / triangle[column][column]
    solved = spread(weights[0]) * basis[0]
    for i in range(1, ITERS):
        solved = solved + spread(weights[i]) * basis[i]
    out_ref[...] = solved
    for column in range(ITERS):
        picture = zero
        for i in range(column + 2):
            picture = jnp.where(lanes == i, raw_columns[column][i], picture)
        hess_ref[column] = picture[0:systems, 0 : ITERS + 1]
    others = pl.ds(0, n - 1)
    remote(asked.at[others], asked.at[others], ask_send, ask_recv, home).wait_send()
    for column in range(ITERS):
        remote(
            outgoing.at[column, others],
            incoming.at[column, others],
            send_sem.at[column],
            recv_sem.at[column, 0],
            home,
        ).wait_send()
    for turn in range(ITERS + 1):
        all_sums(turn).wait_send()


def rotate(column, rotations, triangle, target):
    column = list(column)
    for i, (cosine, sine) in enumerate(rotations):
        first, second = column[i], column[i + 1]
        column[i] = cosine * first + sine * second
        column[i + 1] = cosine * second - sine * first
    last = len(column) - 2
    first, second = column[last], column[last + 1]
    radius = jnp.sqrt(first * first + second * second)
    cosine, sine = first / radius, second / radius
    rotations.append((cosine, sine))
    column[last] = radius
    triangle.append(column[: last + 1])
    leading = target[last]
    target[last] = cosine * leading
    target.append(-sine * leading)


def hand_on(solved_ref, picture_ref, out_ref, hess_ref):
    out_ref[...] = solved_ref[...]
    hess_ref[...] = picture_ref[...]


def on_device(tile_values, tile_row, tile_slot, tile_count, requests, right_side):
    n = lax.axis_size("rows")
    total, size, _ = tile_values.shape
    blocks, systems, _ = right_side.shape
    rows = 2 * systems
    height = blocks * systems
    low = next(part for part in (8, 4, 2, 1) if n % part == 0)
    chunk = 16 if total % 16 == 0 else 1
    smem = pltpu.SMEM
    hbm = pl.BlockSpec(memory_space=pl.ANY)
    vmem = pl.BlockSpec(memory_space=pltpu.VMEM)
    dma = pltpu.SemaphoreType.DMA
    solved, picture = pl.pallas_call(
        functools.partial(kernel, n, low, chunk, min(3, total // chunk)),
        out_shape=(
            jax.ShapeDtypeStruct((height, size), f32),
            jax.ShapeDtypeStruct((ITERS, systems, ITERS + 1), f32),
        ),
        in_specs=[hbm] * 6,
        out_specs=(vmem, vmem),
        scratch_shapes=[
            pltpu.VMEM((total, size, size), f32),
            pltpu.VMEM((total, 2 * size, size), bf16),
            pltpu.VMEM((height, total * rows), f32),
            pltpu.VMEM((1, total), jnp.int32),
            smem((1,), jnp.int32),
            smem((total,), jnp.int32),
            smem((1, n), jnp.int32),
            smem((n, 1, n), jnp.int32),
            pltpu.VMEM((ITERS, n, systems, size), f32),
            pltpu.VMEM((ITERS, n, systems, size), f32),
            pltpu.VMEM((ITERS + 1, 1, size), f32),
            pltpu.VMEM((ITERS + 1, n, 1, size), f32),
            pltpu.VMEM((ITERS + 1, height, size), f32),
            pltpu.VMEM((ITERS, height, size), f32),
            pltpu.VMEM((blocks + n, rows, size), f32),
            pltpu.VMEM((total * rows, size), bf16),
            pltpu.VMEM((total * rows, size), bf16),
            dma((total // chunk,)),
            dma((5,)),
            dma,
            dma,
            dma((ITERS,)),
            dma((ITERS, n)),
            dma((ITERS + 1,)),
            dma((ITERS + 1,)),
        ],
        compiler_params=pltpu.CompilerParams(
            collective_id=0, has_side_effects=True, vmem_limit_bytes=60 * 1024 * 1024
        ),
        name="cycle",
    )(
        tile_values,
        tile_row.reshape(1, total),
        tile_count,
        tile_slot,
        requests.reshape(1, n),
        right_side.reshape(height, size),
    )
    solved, picture = pl.pallas_call(
        hand_on,
        out_shape=(
            jax.ShapeDtypeStruct(solved.shape, f32),
            jax.ShapeDtypeStruct(picture.shape, f32),
        ),
        in_specs=[vmem, vmem],
        out_specs=(vmem, vmem),
        name="hand_on",
    )(solved, picture)
    return solved.reshape(blocks, systems, size), jnp.transpose(picture, (1, 2, 0))


def solution(mesh):
    return jax.shard_map(
        on_device,
        mesh=mesh,
        in_specs=(
            P("rows", None, None),
            P("rows"),
            P("rows"),
            P("rows"),
            P("rows", None, None),
            P("rows", None, None),
        ),
        out_specs=(P("rows", None, None), P()),
        check_vma=False,
    )
```

time: 43.4 us -> 37.7 us (0.87)
  Pallas kernels: 41.9 us -> 36.2 us
    pallas_call x1, Pallas kernels: 40.5 us -> 34.9 us  [on_device(): pl.pallas_call(functools.partial(kernel, n, low, chunk, min(3, total // c...]
where the time goes in v1:
time: 37.7 us; the launch traced here: 37.5 us
  Pallas kernels  36.2 us (96%)
  between operations  1.28 us (3%)
    pallas_call x1, Pallas kernels, on_device(): pl.pallas_call(functools.partial(kernel, n, low, chunk, min(3, total // c...  34.9 us
    pallas_call x1, Pallas kernels, on_device(): pl.pallas_call(hand_on, out_shape=(jax.ShapeDtypeStruct(solved.shape, f32...  1.38 us

profile of v1, /device:TPU:0, one launch (start us, length us, event | category | flops | bytes accessed | tf_op | source)
XLA Modules:
  0.0 37.5 jit_solution(10768171263759269846)
XLA Ops:
  1.3 34.9 %cycle.1 = (f32[64,128]{1,0:T(8,128)}, f32[3,4,4]{2,1,0:T(4,128)}) custom-call(f32[112,128,128]{2,1,0:T(8,128)} %tile_hbm.1, s32[1,112]{1,0:T(1,128)} %bitcast.6, s32[1]{0:T(128)S(6)} %copy.8.count_hbm, s32[112]{0:T(128)} %slot_hbm.1, s32[1,32]{1,0:T(1,128)} %bitcast.7, f32[64,128]{1,0:T(8,128)} %bitcast.5), custom_call_target="tpu_custom_call" | custom-call | tf_op jit(solution)/shard_map/cycle/pallas_call | solution.py:454
  36.1 1.4 %hand_on.1 = (f32[64,128]{1,0:T(8,128)}, f32[3,4,4]{2,1,0:T(4,128)}) custom-call(f32[64,128]{1,0:T(8,128)} %get-tuple-element.6.solved_ref, f32[3,4,4]{2,1,0:T(4,128)} %get-tuple-element.7.picture_ref), custom_call_target="tpu_custom_call" | custom-call | tf_op jit(solution)/shard_map/hand_on/pallas_call | solution.py:501

commit v2 on v1

v2 whole, which is shorter than its diff:
```python
import functools

import jax
import jax.numpy as jnp
from jax import lax
from jax.experimental import pallas as pl
from jax.experimental.pallas import tpu as pltpu
from jax.sharding import PartitionSpec as P

ITERS = 3
LOADS = 5
MESH = pl.DeviceIdType.MESH
epsilon = 1e-06
f32 = jnp.float32
bf16 = jnp.bfloat16


def split(x):
    high = x.astype(bf16).astype(f32)
    return high, x - high


def dot(a, b):
    return lax.dot_general(a, b, (((1,), (0,)), ((), ())), preferred_element_type=f32)


def twice(x):
    return jnp.concatenate([x, x], axis=0)


def flip(value, mask, bits):
    result = 0
    for bit in range(bits):
        a = lax.rem(value // 2**bit, 2)
        b = mask // 2**bit % 2 if isinstance(mask, int) else lax.rem(mask // 2**bit, 2)
        result = result + (a + b - 2 * a * b) * 2**bit
    return result


def kernel(
    n,
    low,
    bounds,
    early,
    tile_hbm,
    row_hbm,
    count_hbm,
    slot_hbm,
    request_hbm,
    right_hbm,
    out_ref,
    hess_ref,
    tiles,
    parts,
    selector,
    row_ref,
    count_ref,
    slot_ref,
    request_ref,
    asked,
    outgoing,
    incoming,
    sums_out,
    sums_in,
    own,
    basis,
    table,
    products,
    solving,
    local_sem,
    ask_recv,
    recv_sem,
    sums_recv,
):
    me = lax.axis_index("rows")
    total, size, _ = tiles.shape
    _, height, _ = own.shape
    systems = outgoing.shape[2]
    blocks = height // systems
    rows = 2 * systems
    statics = blocks + n
    batch = size // rows
    far = n // low
    far_bits, low_bits = far.bit_length() - 1, low.bit_length() - 1
    group_of_me, place = me // low, lax.rem(me, low)
    beside = [flip(place, step, low_bits) for step in range(low)]

    def across(step):
        if far == 2**far_bits:
            return flip(group_of_me, step, far_bits) * low
        return lax.rem(group_of_me + step, far) * low

    home = group_of_me * low

    def far_first(body, top=far, bottom=0):
        def run(index, carry):
            group = across(top - 1 - index)
            for step in reversed(range(low)):
                body(group + beside[step])
            return carry

        stop = max(bottom, 1)
        if top - stop <= 3:
            for index in range(top - stop):
                run(index, 0)
        else:
            lax.fori_loop(0, top - stop, run, 0)
        if bottom == 0:
            for step in reversed(range(1, low)):
                body(home + beside[step])

    ask_send, send_sem, sums_send = (local_sem.at[index] for index in range(3))

    def remote(source, target, send, recv, peer):
        return pltpu.make_async_remote_copy(
            src_ref=source,
            dst_ref=target,
            send_sem=send,
            recv_sem=recv,
            device_id=(peer,),
            device_id_type=MESH,
        )

    tile_copies = [
        pltpu.make_async_copy(
            tile_hbm.at[pl.ds(begin, end - begin)],
            tiles.at[pl.ds(begin, end - begin)],
            local_sem.at[LOADS + index],
        )
        for index, (begin, end) in enumerate(zip(bounds[:-1], bounds[1:]))
    ]
    tile_copies[0].start()
    barrier = pltpu.get_barrier_semaphore()
    far_first(
        lambda peer: pl.semaphore_signal(barrier, inc=1, device_id=(peer,), device_id_type=MESH)
    )

    loads = [
        pltpu.make_async_copy(source, target, local_sem.at[index])
        for index, (source, target) in enumerate(
            [
                (request_hbm, request_ref),
                (row_hbm, row_ref),
                (count_hbm, count_ref),
                (slot_hbm, slot_ref),
                (right_hbm, own.at[0]),
            ]
        )
    ]
    for load in loads:
        load.start()
    for copy in tile_copies[1:]:
        copy.start()

    def split_tiles(index):
        tile_copies[index].wait()

        def split_tile(tile, carry):
            high, low_part = split(tiles[tile].T)
            parts[tile, 0:size, :] = high.astype(bf16)
            parts[tile, size : 2 * size, :] = low_part.astype(bf16)
            return carry

        lax.fori_loop(bounds[index], bounds[index + 1], split_tile, 0, unroll=4)

    for index in range(early):
        split_tiles(index)
    pl.semaphore_wait(barrier, n - 1)
    for load in loads:
        load.wait()
    far_first(
        lambda peer: remote(request_ref, asked.at[me], ask_send, ask_recv, peer).start()
    )
    for index in range(early, len(tile_copies)):
        split_tiles(index)

    lane = lax.broadcasted_iota(jnp.int32, (1, total), 1)
    live_row = jnp.where(lane < count_ref[0], row_ref[...], blocks)
    wide = total * rows
    from_tile = lax.broadcasted_iota(jnp.int32, (total, wide), 0)
    to_column = lax.broadcasted_iota(jnp.int32, (total, wide), 1)
    expand = jnp.where(to_column // rows == from_tile, 1.0, 0.0).astype(bf16)
    row_of = dot(jnp.broadcast_to(live_row.astype(f32), (8, total)).astype(bf16), expand)[0:1]
    k_row = lax.broadcasted_iota(jnp.int32, (height, size), 0)
    q_col = lax.broadcasted_iota(jnp.int32, (height, size), 1)
    same_system = k_row % systems == q_col % systems
    block = (k_row // systems).astype(f32)
    for part in range(total // batch):
        here = row_of[:, part * size : (part + 1) * size]
        fits = same_system & (jnp.broadcast_to(here, (height, size)) == block)
        mask = jnp.where(fits, 1.0, 0.0).astype(bf16)
        selector[part, :, 0:size] = mask
        selector[part, :, size : 2 * size] = mask

    sub = lax.broadcasted_iota(jnp.int32, (rows, size), 0)
    lanes = lax.broadcasted_iota(jnp.int32, (rows, size), 1)
    system_of = sub % systems

    def send_blocks(column, top, bottom):
        def send(peer):
            start = asked[peer, 0, me] * systems
            outgoing[column, peer] = own[column, pl.ds(start, systems), :]
            remote(
                outgoing.at[column, peer],
                incoming.at[column, me],
                send_sem,
                recv_sem.at[column % 2, group_of_me],
                peer,
            ).start()

        far_first(send, top, bottom)

    def fold(x, y):
        product = (x * y).reshape(height // rows, rows, size)
        return jnp.sum(jnp.sum(product, axis=0), axis=1, keepdims=True)

    def send_sums(turn, sums):
        packed = jnp.zeros((rows, size), f32)
        for position, entry in enumerate(sums):
            packed = packed + jnp.where(lanes == rows * position + sub, entry, 0.0)
        packed = jnp.sum(packed, axis=0, keepdims=True)
        sums_out[turn] = packed
        sums_in[turn, me] = packed
        far_first(
            lambda peer: remote(
                sums_out.at[turn],
                sums_in.at[turn, me],
                sums_send,
                sums_recv.at[turn % 2],
                peer,
            ).start()
        )

    def all_sums(turn):
        others = pl.ds(0, n - 1)
        return remote(
            sums_in.at[turn, others],
            sums_in.at[turn, others],
            sums_send,
            sums_recv.at[turn % 2],
            home + beside[1],
        )

    def arrive_sums(turn, count):
        all_sums(turn).wait_recv()
        whole = jnp.sum(sums_in[turn], axis=0)
        whole = jnp.broadcast_to(whole, (rows, size))
        return [
            jnp.broadcast_to(
                jnp.sum(
                    jnp.where(
                        (lanes // rows == position) & (lanes % systems == system_of), whole, 0.0
                    ),
                    axis=1,
                    keepdims=True,
                ),
                (rows, size),
            )
            for position in range(count)
        ]

    def fill(slot, raw):
        high, rest = split(twice(raw))
        table[slot] = jnp.where(sub < systems, high, rest)

    def multiply(first, count):
        for pair in range(count // 2):
            both = []
            for side in range(2):
                tile, slot = first(2 * pair + side)
                x = table[slot].astype(bf16)
                both.append(dot(jnp.concatenate([x, x], axis=1), parts[tile]))
            y = jnp.concatenate(both, axis=0)
            high, rest = split(y)
            tile, _ = first(2 * pair)
            if isinstance(tile, int):
                part, start = tile // batch, tile % batch * rows
            else:
                part, start = tile // batch, pl.multiple_of(lax.rem(tile, batch) * rows, 2 * rows)
            products[part, pl.ds(start, 2 * rows), :] = high.astype(bf16)
            products[part, pl.ds(size + start, 2 * rows), :] = rest.astype(bf16)

    def near_tiles(column):
        for block in range(blocks):
            fill(block, own[column, pl.ds(block * systems, systems), :])
        multiply(lambda index: (index, index), blocks)

    def group_tiles(column, group):
        for index in range(low):
            fill(blocks + group + index, incoming[column, group + index])
        multiply(lambda index: (blocks + group + index, blocks + group + index), low)

    def arrive(column, step):
        group = across(step)
        count = low - 1 if isinstance(step, int) and step == 0 else low
        remote(
            outgoing.at[column, pl.ds(group, count)],
            incoming.at[column, pl.ds(group, count)],
            send_sem,
            recv_sem.at[column % 2, group // low],
            home + beside[1],
        ).wait_recv()

    def static_tiles(column):
        near_tiles(column)
        incoming[column, me] = own[column, pl.ds(request_ref[0, me] * systems, systems), :]
        arrive(column, 0)
        group_tiles(column, home)

        def run(step, carry):
            arrive(column, step)
            group_tiles(column, across(step))
            return carry

        if far <= 4:
            for step in range(1, far - 1):
                run(step, 0)
        else:
            lax.fori_loop(1, far - 1, run, 0)
        arrive(column, far - 1)

    def select():
        result = dot(selector[0], products[0])
        for part in range(1, total // batch):
            result = result + dot(selector[part], products[part])
        return result

    def spread(value):
        return jnp.tile(value, (height // rows, 1))

    zero = jnp.zeros((rows, size), f32)
    remote(asked.at[pl.ds(0, n - 1)], asked.at[pl.ds(0, n - 1)], ask_send, ask_recv, home + beside[1]).wait_recv()
    middle = far // 2
    send_blocks(0, far, middle)
    send_sums(0, [fold(own[0], own[0])])
    send_blocks(0, middle, 0)

    gram = {}
    triangle = []
    raw_columns = []
    rotations = []
    target = []
    coefficients = []
    extras = total - statics

    def inner(i, j):
        return gram[(min(i, j), max(i, j))]

    def orthogonalize(column, summed):
        if column == 0:
            beta = jnp.sqrt(summed[0] + epsilon)
            scale = 1.0 / beta
            gram[(0, 0)] = summed[0] * scale * scale
            target.append(beta)
            return [], scale
        count = column
        values, square = project(column, summed)
        length = jnp.sqrt(square)
        scale = 1.0 / length
        for i in range(count):
            value = summed[i]
            for earlier in range(count):
                value = value - values[earlier] * inner(earlier, i)
            gram[(i, count)] = value * scale
        gram[(count, count)] = (square - epsilon) * scale * scale
        raw_columns.append(values + [length])
        return values, scale

    def project(count, summed):
        values = []
        for i in range(count):
            value = summed[i]
            for earlier in range(i):
                value = value - values[earlier] * inner(earlier, i)
            values.append(value)
        residual = summed[count]
        for i in range(count):
            residual = residual - 2.0 * values[i] * summed[i]
        for i in range(count):
            for j in range(count):
                residual = residual + values[i] * values[j] * inner(i, j)
        return values, jnp.maximum(residual, 0.0) + epsilon

    for column in range(ITERS):
        static_tiles(column)
        group_tiles(column, across(far - 1))
        multiply(lambda index: (statics + index, slot_ref[statics + index]), extras)
        summed = arrive_sums(column, column + 1)
        values, scale = orthogonalize(column, summed)
        vector = own[column]
        for i, value in enumerate(values):
            vector = vector - spread(value) * basis[i]
        vector = vector * spread(scale)
        basis[column] = vector
        candidate = select()
        for i, value in enumerate(values):
            candidate = candidate - spread(value) * own[i + 1]
        candidate = candidate * spread(scale)
        own[column + 1] = candidate
        if column + 1 < ITERS:
            send_blocks(column + 1, far, middle)
        sums = [fold(candidate, basis[i]) for i in range(column + 1)]
        sums.append(fold(candidate, candidate))
        send_sums(column + 1, sums)
        if column + 1 < ITERS:
            send_blocks(column + 1, middle, 0)
        if column >= 1:
            rotate(raw_columns[column - 1], rotations, triangle, target)

    last = ITERS - 1
    inverse = [1.0 / triangle[column][column] for column in range(last)]

    def back(entries):
        found = [None] * last
        for column in reversed(range(last)):
            value = entries[column]
            for later in range(column + 1, last):
                value = value - triangle[later][column] * found[later]
            found[column] = value * inverse[column]
        return found

    before = back(target[0:last])
    start = spread(before[0]) * basis[0]
    for i in range(1, last):
        start = start + spread(before[i]) * basis[i]
    solving[...] = start
    summed = arrive_sums(ITERS, ITERS + 1)
    values, square = project(ITERS, summed)
    entries = list(values)
    for i, (cosine, sine) in enumerate(rotations):
        first, second = entries[i], entries[i + 1]
        entries[i] = cosine * first + sine * second
        entries[i + 1] = cosine * second - sine * first
    lead = entries[last]
    weight = lead * target[last] / (lead * lead + square)
    along = back(entries[0:last])
    solved = solving[...] + spread(weight) * basis[last]
    for i in range(last):
        solved = solved - spread(weight * along[i]) * basis[i]
    out_ref[...] = solved
    raw_columns.append(values + [jnp.sqrt(square)])
    for column in range(ITERS):
        picture = zero
        for i in range(column + 2):
            picture = jnp.where(lanes == i, raw_columns[column][i], picture)
        hess_ref[column] = picture[0:systems, 0 : ITERS + 1]
    others = pl.ds(0, n - 1)
    peer = home + beside[1]
    remote(asked.at[others], asked.at[others], ask_send, ask_recv, peer).wait_send()
    remote(
        outgoing.at[:, others], incoming.at[:, others], send_sem, recv_sem.at[0, 0], peer
    ).wait_send()
    remote(
        sums_in.at[:, others], sums_in.at[:, others], sums_send, sums_recv.at[0], peer
    ).wait_send()


def rotate(column, rotations, triangle, target):
    column = list(column)
    for i, (cosine, sine) in enumerate(rotations):
        first, second = column[i], column[i + 1]
        column[i] = cosine * first + sine * second
        column[i + 1] = cosine * second - sine * first
    last = len(column) - 2
    first, second = column[last], column[last + 1]
    radius = jnp.sqrt(first * first + second * second)
    cosine, sine = first / radius, second / radius
    rotations.append((cosine, sine))
    column[last] = radius
    triangle.append(column[: last + 1])
    leading = target[last]
    target[last] = cosine * leading
    target.append(-sine * leading)


def hand_on(solved_ref, picture_ref, out_ref, hess_ref, sem):
    copies = [
        pltpu.make_async_copy(solved_ref, out_ref, sem.at[0]),
        pltpu.make_async_copy(picture_ref, hess_ref, sem.at[1]),
    ]
    for copy in copies:
        copy.start()
    for copy in copies:
        copy.wait()


def on_device(tile_values, tile_row, tile_slot, tile_count, requests, right_side):
    n = lax.axis_size("rows")
    total, size, _ = tile_values.shape
    blocks, systems, _ = right_side.shape
    rows = 2 * systems
    height = blocks * systems
    low = next(part for part in (8, 4, 2, 1) if n % part == 0)
    begin = blocks + blocks
    bounds = (0, blocks, begin, (begin + total) // 2, total)
    smem = pltpu.SMEM
    hbm = pl.BlockSpec(memory_space=pl.ANY)
    vmem = pl.BlockSpec(memory_space=pltpu.VMEM)
    dma = pltpu.SemaphoreType.DMA
    solved, picture = pl.pallas_call(
        functools.partial(kernel, n, low, bounds, 2),
        out_shape=(
            pltpu.VMEM((height, size), f32),
            pltpu.VMEM((ITERS, systems, ITERS + 1), f32),
        ),
        in_specs=[hbm] * 6,
        out_specs=(vmem, vmem),
        scratch_shapes=[
            pltpu.VMEM((total, size, size), f32),
            pltpu.VMEM((total, 2 * size, size), bf16),
            pltpu.VMEM((total * rows // size, height, 2 * size), bf16),
            pltpu.VMEM((1, total), jnp.int32),
            smem((1,), jnp.int32),
            smem((total,), jnp.int32),
            smem((1, n), jnp.int32),
            smem((n, 1, n), jnp.int32),
            pltpu.VMEM((ITERS, n, systems, size), f32),
            pltpu.VMEM((ITERS, n, systems, size), f32),
            pltpu.VMEM((ITERS + 1, 1, size), f32),
            pltpu.VMEM((ITERS + 1, n, 1, size), f32),
            pltpu.VMEM((ITERS + 1, height, size), f32),
            pltpu.VMEM((ITERS, height, size), f32),
            pltpu.VMEM((blocks + n, rows, size), f32),
            pltpu.VMEM((total * rows // size, 2 * size, size), bf16),
            pltpu.VMEM((height, size), f32),
            dma((LOADS + len(bounds) - 1,)),
            dma,
            dma((2, n // low)),
            dma((2,)),
        ],
        compiler_params=pltpu.CompilerParams(
            collective_id=0, has_side_effects=True, vmem_limit_bytes=60 * 1024 * 1024
        ),
        name="cycle",
    )(
        tile_values,
        tile_row.reshape(1, total),
        tile_count,
        tile_slot,
        requests.reshape(1, n),
        right_side.reshape(height, size),
    )
    solved, picture = pl.pallas_call(
        hand_on,
        out_shape=(
            jax.ShapeDtypeStruct(solved.shape, f32),
            jax.ShapeDtypeStruct(picture.shape, f32),
        ),
        in_specs=[hbm, hbm],
        out_specs=(hbm, hbm),
        scratch_shapes=[dma((2,))],
        compiler_params=pltpu.CompilerParams(vmem_limit_bytes=1 << 20),
        name="hand_on",
    )(solved, picture)
    return solved.reshape(blocks, systems, size), jnp.transpose(picture, (1, 2, 0))


def solution(mesh):
    return jax.shard_map(
        on_device,
        mesh=mesh,
        in_specs=(
            P("rows", None, None),
            P("rows"),
            P("rows"),
            P("rows"),
            P("rows", None, None),
            P("rows", None, None),
        ),
        out_specs=(P("rows", None, None), P()),
        check_vma=False,
    )
```

time: 37.7 us -> 34.6 us (0.918)
  Pallas kernels: 36.2 us -> 33.1 us
    pallas_call x1, Pallas kernels: 34.9 us -> 32.5 us  [on_device(): pl.pallas_call(functools.partial(kernel, n, low, bounds, 2), out_shape=(p...]
    pallas_call x1, Pallas kernels: 1.38 us -> 0.64 us  [on_device(): pl.pallas_call(hand_on, out_shape=(jax.ShapeDtypeStruct(solved.shape, f32...]
where the time goes in v2:
time: 34.6 us; the launch traced here: 34.4 us
  Pallas kernels  33.1 us (96%)
  between operations  1.28 us (4%)
    pallas_call x1, Pallas kernels, on_device(): pl.pallas_call(functools.partial(kernel, n, low, bounds, 2), out_shape=(p...  32.5 us

profile of v2, /device:TPU:0, one launch (start us, length us, event | category | flops | bytes accessed | tf_op | source)
XLA Modules:
  0.0 34.4 jit_solution(10636757487439482358)
XLA Ops:
  1.3 32.5 %cycle.1 = (f32[64,128]{1,0:T(8,128)S(1)}, f32[3,4,4]{2,1,0:T(4,128)S(1)}) custom-call(f32[112,128,128]{2,1,0:T(8,128)} %tile_hbm.1, s32[1,112]{1,0:T(1,128)} %bitcast.6, s32[1]{0:T(128)S(6)} %copy.8.count_hbm, s32[112]{0:T(128)} %slot_hbm.1, s32[1,32]{1,0:T(1,128)} %bitcast.7, f32[64,128]{1,0:T(8,128)} %bitcast.5), custom_call_target="tpu_custom_call" | custom-call | tf_op jit(solution)/shard_map/cycle/pallas_call | solution.py:500
  33.8 0.6 %hand_on.1 = (f32[64,128]{1,0:T(8,128)}, f32[3,4,4]{2,1,0:T(4,128)}) custom-call(f32[64,128]{1,0:T(8,128)S(1)} %get-tuple-element.6.solved_ref, f32[3,4,4]{2,1,0:T(4,128)S(1)} %get-tuple-element.7.picture_ref), custom_call_target="tpu_custom_call" | custom-call | tf_op jit(solution)/shard_map/hand_on/pallas_call | solution.py:543

commit v3 on v2

--- a/solution.py
+++ b/solution.py
@@ -85,7 +85,12 @@
     group_of_me, place = me // low, lax.rem(me, low)
     beside = [flip(place, step, low_bits) for step in range(low)]
 
+    quarter = group_of_me * 4 // far
+    swap = jnp.where((quarter == 1) | (quarter == 2), 1, 0) if far % 4 == 0 else 0
+
     def across(step):
+        if far % 4 == 0 and isinstance(step, int) and step >= far - 2:
+            step = step - swap if step == far - 1 else step + swap
         if far == 2**far_bits:
             return flip(group_of_me, step, far_bits) * low
         return lax.rem(group_of_me + step, far) * low
@@ -129,7 +134,6 @@
         )
         for index, (begin, end) in enumerate(zip(bounds[:-1], bounds[1:]))
     ]
-    tile_copies[0].start()
     barrier = pltpu.get_barrier_semaphore()
     far_first(
         lambda peer: pl.semaphore_signal(barrier, inc=1, device_id=(peer,), device_id_type=MESH)
@@ -147,6 +151,7 @@
             ]
         )
     ]
+    tile_copies[0].start()
     for load in loads:
         load.start()
     for copy in tile_copies[1:]:
@@ -166,11 +171,12 @@
     for index in range(early):
         split_tiles(index)
     pl.semaphore_wait(barrier, n - 1)
-    for load in loads:
-        load.wait()
+    loads[0].wait()
     far_first(
         lambda peer: remote(request_ref, asked.at[me], ask_send, ask_recv, peer).start()
     )
+    for load in loads[1:]:
+        load.wait()
     for index in range(early, len(tile_copies)):
         split_tiles(index)
 
@@ -330,10 +336,8 @@
 
     zero = jnp.zeros((rows, size), f32)
     remote(asked.at[pl.ds(0, n - 1)], asked.at[pl.ds(0, n - 1)], ask_send, ask_recv, home + beside[1]).wait_recv()
-    middle = far // 2
-    send_blocks(0, far, middle)
+    send_blocks(0, far, 0)
     send_sums(0, [fold(own[0], own[0])])
-    send_blocks(0, middle, 0)
 
     gram = {}
     triangle = []
@@ -398,12 +402,10 @@
         candidate = candidate * spread(scale)
         own[column + 1] = candidate
         if column + 1 < ITERS:
-            send_blocks(column + 1, far, middle)
+            send_blocks(column + 1, far, 0)
         sums = [fold(candidate, basis[i]) for i in range(column + 1)]
         sums.append(fold(candidate, candidate))
         send_sums(column + 1, sums)
-        if column + 1 < ITERS:
-            send_blocks(column + 1, middle, 0)
         if column >= 1:
             rotate(raw_columns[column - 1], rotations, triangle, target)
 

time: 34.6 us -> 34.4 us (level)
  no operation moved by 1% of the time
where the time goes in v3:
time: 34.4 us; the launch traced here: 34.2 us
  Pallas kernels  32.9 us (96%)
  between operations  1.28 us (4%)
    pallas_call x1, Pallas kernels, on_device(): pl.pallas_call(functools.partial(kernel, n, low, bounds, 2), out_shape=(p...  32.3 us

profile of v3, /device:TPU:0, one launch (start us, length us, event | category | flops | bytes accessed | tf_op | source)
XLA Modules:
  0.0 34.2 jit_solution(2190528440732550097)
XLA Ops:
  1.3 32.3 %cycle.1 = (f32[64,128]{1,0:T(8,128)S(1)}, f32[3,4,4]{2,1,0:T(4,128)S(1)}) custom-call(f32[112,128,128]{2,1,0:T(8,128)} %tile_hbm.1, s32[1,112]{1,0:T(1,128)} %bitcast.6, s32[1]{0:T(128)S(6)} %copy.8.count_hbm, s32[112]{0:T(128)} %slot_hbm.1, s32[1,32]{1,0:T(1,128)} %bitcast.7, f32[64,128]{1,0:T(8,128)} %bitcast.5), custom_call_target="tpu_custom_call" | custom-call | tf_op jit(solution)/shard_map/cycle/pallas_call | solution.py:502
  33.6 0.6 %hand_on.1 = (f32[64,128]{1,0:T(8,128)}, f32[3,4,4]{2,1,0:T(4,128)}) custom-call(f32[64,128]{1,0:T(8,128)S(1)} %get-tuple-element.6.solved_ref, f32[3,4,4]{2,1,0:T(4,128)S(1)} %get-tuple-element.7.picture_ref), custom_call_target="tpu_custom_call" | custom-call | tf_op jit(solution)/shard_map/hand_on/pallas_call | solution.py:545
